TPU v7x, 32 devices: a whole 2x2x4 slice. The times are simulated.
32 devices in a mesh: chain: 32 (over z, y, x, core).
Axes of the slice: x: 2, y: 2, z: 4, core: 2. Of those that a mesh axis runs over, the one named last changes fastest.
Arguments:
- sections: float32 [32, 2, 4, 2, 128, 128], P('chain'), may hold values from -1.2 to 1.2
- probes: float32 [2, 2, 128, 4096], P(None, None, None, 'chain'), may hold values from -6 to 6
Outputs:
- prefixes: float32 [32, 2, 4, 2, 128, 128], P('chain')
- reflected: float32 [2, 2, 128, 4096], P(None, None, None, 'chain')
- transmitted: float32 [2, 2, 128, 4096], P(None, None, None, 'chain')
All inputs are finite; a program needn't handle non-finite values.
Results may differ from a plain program's by a relative error of at most 0.0003.
Values sent between devices are 32-bit elements; how exact they have to be, the bound alone decides.
A program may use at most 128 MiB of HBM per device.

v0:
```python
import functools

import jax
import jax.numpy as jnp
from jax import lax
from jax.experimental import pallas as pl
from jax.experimental.pallas import tpu as pltpu
from jax.sharding import PartitionSpec as P

INV_STEPS = 9
LEFT, BACK, FORE, RIGHT = range(4)
MESH = pl.DeviceIdType.MESH
f32, bf16 = jnp.float32, jnp.bfloat16


def split(x):
    high = x.astype(bf16)
    return high, (x - high.astype(f32)).astype(bf16)


def quarter_turn(block):
    half = block.shape[1] // 2
    return jnp.concatenate([-block[:, half:], block[:, :half]], axis=1)


def embedded(block):
    return split(jnp.concatenate([block, quarter_turn(block)], axis=0))


def product(former, latter):
    rows = former.shape[0]
    high, low = split(former)
    by_high = jnp.dot(jnp.concatenate([high, low], axis=0), latter[0], preferred_element_type=f32)
    by_low = jnp.dot(high, latter[1], preferred_element_type=f32)
    return by_high[:rows] + by_high[rows:] + by_low


def unit(size):
    row = lax.broadcasted_iota(jnp.int32, (size, 2 * size), 0)
    column = lax.broadcasted_iota(jnp.int32, (size, 2 * size), 1)
    return jnp.where(row == column, 1.0, 0.0).astype(f32)


def star(pairs, work, late=None):
    size = work.shape[1] // 2
    for i, (first, second, _) in enumerate(pairs):
        bounce = product(second[LEFT], embedded(first[RIGHT]))
        work[i, :size] = unit(size) + bounce
        work[i, size:] = product(bounce, embedded(bounce))

    def double(_, carry):
        for i in range(len(pairs)):
            both = work[i]
            grown = product(both, embedded(both[size:]))
            work[i, :size] = both[:size] + grown[:size]
            work[i, size:] = grown[size:]
        return carry

    lax.fori_loop(0, INV_STEPS - 2, double, 0)
    if late is not None:
        late()
    for i, (first, second, emit) in enumerate(pairs):
        partial = work[i, :size]
        resolvent = partial + product(partial, embedded(work[i, size:]))
        second_left = second[LEFT]
        fore = embedded(first[FORE])
        back = embedded(second[BACK])
        leading = product(first[BACK], embedded(resolvent))
        inner = product(resolvent, embedded(second_left))
        emit(LEFT, first[LEFT] + product(leading, embedded(product(second_left, fore))))
        through = product(second[FORE], embedded(first[RIGHT]))
        trailing = second[FORE] + product(through, embedded(inner))
        emit(RIGHT, second[RIGHT] + product(trailing, embedded(product(first[RIGHT], back))))
        emit(BACK, product(leading, back))
        emit(FORE, product(trailing, fore))


def kernel(
    n, levels, sections, probes, prefixes, reflected, transmitted,
    arrived, own, stage, before, work, total, leaving,
    swap_sems, stage_send, stage_recv, total_sems, out_send, out_recv,
):
    me = lax.axis_index("chain")
    core = me % 2
    sibling = me + 1 - 2 * core
    size = probes.shape[2]

    def partner(stride):
        return me + stride - 2 * stride * ((me // stride) % 2)

    barrier = pltpu.get_barrier_semaphore()
    for level in range(levels + 1):
        pl.semaphore_signal(barrier, inc=1, device_id=(partner(1 << level),), device_id_type=MESH)
    pl.semaphore_wait(barrier, levels + 1)

    def remote(source, target, send, recv, device):
        return pltpu.make_async_remote_copy(
            src_ref=source, dst_ref=target, send_sem=send, recv_sem=recv, device_id=(device,), device_id_type=MESH
        )

    swap = remote(sections.at[0, 1 - core], arrived, swap_sems.at[0], swap_sems.at[1], sibling)
    swap.start()

    def joined(block):
        return jnp.concatenate([block[0], block[1]], axis=1)

    vacant = jnp.zeros((size, 2 * size), f32)
    for b in range(4):
        own[core, b] = joined(sections[0, core, b])
        before[b] = vacant if b in (LEFT, RIGHT) else unit(size)
    swap.wait()
    for b in range(4):
        own[1 - core, b] = joined(arrived[b])

    def stage_copy(level, stride, block):
        place = stage.at[level, (me // stride) % 2, block]
        return remote(place, place, stage_send.at[level, block], stage_recv.at[level, block], partner(stride))

    def total_copy(k):
        return remote(
            stage.at[levels, 0, (LEFT, FORE)[k]], total.at[k], total_sems.at[0, k], total_sems.at[1, k], sibling
        )

    def emit_stage(level, stride):
        def emit(block, value):
            stage[level, (me // stride) % 2, block] = value

            @pl.when(level < levels)
            def _():
                stage_copy(level, stride, block).start()

            if block in (LEFT, FORE):

                @pl.when(level == levels)
                def _():
                    total_copy((LEFT, FORE).index(block)).start()

        return emit

    def emit_before(block, value):
        before[block] = value

    if levels:
        first_emit = emit_stage(0, 2)
    else:
        first_emit = emit_stage(0, n)
    star([(own.at[0], own.at[1], first_emit)], work)
    pair_slot = (me // 2) % 2 if levels else 0
    for b in range(4):
        own[1, b] = stage[0, pair_slot, b]

    def climb(level, stride):
        lower, upper = stage.at[level, 0], stage.at[level, 1]

        def wait_for(*blocks):
            for block in blocks:
                stage_copy(level, stride, block).wait_recv()

        wait_for(LEFT, RIGHT)
        star([(lower, upper, emit_stage(level + 1, 2 * stride))], work, lambda: wait_for(BACK, FORE))

        @pl.when((me // stride) % 2 == 1)
        def _():
            star([(lower, before, emit_before)], work)

        return 2 * stride

    lax.fori_loop(0, levels, climb, jnp.int32(2))

    def probe(frequency, whole):
        field = embedded(joined(probes[frequency]))
        result = product(whole, field)
        for k, out in enumerate((reflected, transmitted)):
            out[frequency, 0] = result[k * size : (k + 1) * size, :size]
            out[frequency, 1] = result[k * size : (k + 1) * size, size:]

    probe(core, jnp.concatenate([stage[levels, 0, LEFT], stage[levels, 0, FORE]], axis=0))

    def out_copy(block):
        return remote(
            leaving.at[block], prefixes.at[0, core, block], out_send.at[block], out_recv.at[block], sibling
        )

    def emit_away(block, value):
        leaving[block, 0] = value[:, :size]
        leaving[block, 1] = value[:, size:]
        out_copy(block).start()

    def emit_own(block, value):
        prefixes[0, core, block, 0] = value[:, :size]
        prefixes[0, core, block, 1] = value[:, size:]

    star([(before, own.at[1 - core], emit_away), (before, own.at[core], emit_own)], work)

    for k in range(2):
        total_copy(k).wait()
    probe(1 - core, jnp.concatenate([total[0], total[1]], axis=0))

    def drain(level, stride):
        for block in range(4):
            stage_copy(level, stride, block).wait_send()
        return 2 * stride

    lax.fori_loop(0, levels, drain, jnp.int32(2))
    for block in range(4):
        out_copy(block).wait()


def solution(mesh):
    n = mesh.shape["chain"]
    levels = (n // 2 - 1).bit_length()

    def local(sections, probes):
        size = probes.shape[2]
        wide = (size, 2 * size)
        dma = pltpu.SemaphoreType.DMA
        vmem = pl.BlockSpec(memory_space=pltpu.VMEM)
        return pl.pallas_call(
            functools.partial(kernel, n, levels),
            out_shape=tuple(jax.ShapeDtypeStruct(a.shape, f32) for a in (sections, probes, probes)),
            in_specs=[vmem] * 2,
            out_specs=(vmem,) * 3,
            scratch_shapes=[
                pltpu.VMEM(sections.shape[2:], f32),
                pltpu.VMEM((2, 4) + wide, f32),
                pltpu.VMEM((levels + 1, 2, 4) + wide, f32),
                pltpu.VMEM((4,) + wide, f32),
                pltpu.VMEM((2, 2 * size, 2 * size), f32),
                pltpu.VMEM((2,) + wide, f32),
                pltpu.VMEM(sections.shape[2:], f32),
                dma((2,)),
                dma((max(levels, 1), 4)),
                dma((max(levels, 1), 4)),
                dma((2, 2)),
                dma((4,)),
                dma((4,)),
            ],
            compiler_params=pltpu.CompilerParams(
                collective_id=0, has_side_effects=True, vmem_limit_bytes=48 * 1024 * 1024
            ),
        )(sections, probes)

    placed = (P("chain", None, None, None, None, None), P(None, None, None, "chain"))
    return jax.shard_map(
        local, mesh=mesh, in_specs=placed, out_specs=(placed[0], placed[1], placed[1]), check_vma=False
    )
```

profile of v0, /device:TPU:25, one launch (start us, length us, event | category | flops | bytes accessed | tf_op | source)
XLA Modules:
  0.0 88.6 jit_solution(8698195218576192451)
XLA Ops:
  0.6 0.0 copy-start
  0.6 1.2 %copy-done = f32[1,2,4,2,128,128]{5,4,3,2,1,0:T(8,128)S(1)} copy-done((f32[1,2,4,2,128,128]{5,4,3,2,1,0:T(8,128)S(1)}, f32[1,2,4,2,128,128]{5,4,3,2,1,0:T(8,128)}, u32[]{:S(2)}) %copy-start) | copy-done | bytes 1048600
  1.9 0.0 copy-start.1
  1.9 0.9 %copy-done.1 = f32[2,2,128,128]{3,2,1,0:T(8,128)S(1)} copy-done((f32[2,2,128,128]{3,2,1,0:T(8,128)S(1)}, f32[2,2,128,128]{3,2,1,0:T(8,128)}, u32[]{:S(2)}) %copy-start.1) | copy-done | bytes 262168
  2.8 83.4 %shard_map.49 = (f32[1,2,4,2,128,128]{5,4,3,2,1,0:T(8,128)S(1)}, f32[2,2,128,128]{3,2,1,0:T(8,128)S(1)}, f32[2,2,128,128]{3,2,1,0:T(8,128)S(1)}) custom-call(f32[1,2,4,2,128,128]{5,4,3,2,1,0:T(8,128)S(1)} %copy-done, f32[2,2,128,128]{3,2,1,0:T(8,128)S(1)} %copy-done.1), custom_call_target="tpu_custom_call" | custom-call | tf_op jit(solution)/shard_map/pallas_call | solution.py:218
  86.2 1.0 %copy.8 = f32[1,2,4,2,128,128]{5,4,3,2,1,0:T(8,128)} copy(f32[1,2,4,2,128,128]{5,4,3,2,1,0:T(8,128)S(1)} %get-tuple-element.6) | data formatting | bytes 2097152
  87.2 0.7 copy.9
  87.9 0.7 copy.10
Async XLA Ops:
  0.6 1.2 %copy-start = (f32[1,2,4,2,128,128]{5,4,3,2,1,0:T(8,128)S(1)}, f32[1,2,4,2,128,128]{5,4,3,2,1,0:T(8,128)}, u32[]{:S(2)}) copy-start(f32[1,2,4,2,128,128]{5,4,3,2,1,0:T(8,128)} %sections.1) | copy-start | bytes 3145732
  1.9 0.9 %copy-start.1 = (f32[2,2,128,128]{3,2,1,0:T(8,128)S(1)}, f32[2,2,128,128]{3,2,1,0:T(8,128)}, u32[]{:S(2)}) copy-start(f32[2,2,128,128]{3,2,1,0:T(8,128)} %probes.1) | copy-start | bytes 786436
where the time goes:
time: 88.8 us; the launch traced here: 88.6 us
  Pallas kernels  83.4 us (94%)
  local copies, waits for them, and re-layouts  4.54 us (5%)
    pallas_call x1, Pallas kernels, local(): pl.pallas_call(functools.partial(kernel, n, levels), out_shape=tuple((jax...  83.4 us
    unnamed x7, local copies, waits for them, and re-layouts  4.54 us

commit v1 on v0

--- a/solution.py
+++ b/solution.py
@@ -41,7 +41,7 @@
     return jnp.where(row == column, 1.0, 0.0).astype(f32)
 
 
-def star(pairs, work, late=None):
+def star(pairs, work, early=None, middle=None, late=None):
     size = work.shape[1] // 2
     for i, (first, second, _) in enumerate(pairs):
         bounce = product(second[LEFT], embedded(first[RIGHT]))
@@ -56,7 +56,12 @@
             work[i, size:] = grown[size:]
         return carry
 
-    lax.fori_loop(0, INV_STEPS - 2, double, 0)
+    if early is not None:
+        early()
+    lax.fori_loop(0, 2, double, 0)
+    if middle is not None:
+        middle()
+    lax.fori_loop(2, INV_STEPS - 2, double, 0)
     if late is not None:
         late()
     for i, (first, second, emit) in enumerate(pairs):
@@ -78,9 +83,10 @@
 def kernel(
     n, levels, sections, probes, prefixes, reflected, transmitted,
     arrived, own, stage, before, work, total, leaving,
-    swap_sems, stage_send, stage_recv, total_sems, out_send, out_recv,
+    swap_sems, stage_send, stage_recv, pass_send, pass_recv, relay_send, total_sems, out_send, out_recv,
 ):
     me = lax.axis_index("chain")
+    relaying = int(levels >= 3)
     core = me % 2
     sibling = me + 1 - 2 * core
     size = probes.shape[2]
@@ -91,7 +97,10 @@
     barrier = pltpu.get_barrier_semaphore()
     for level in range(levels + 1):
         pl.semaphore_signal(barrier, inc=1, device_id=(partner(1 << level),), device_id_type=MESH)
-    pl.semaphore_wait(barrier, levels + 1)
+    if relaying:
+        facing = partner(n // 2) + partner(n // 4) - me
+        pl.semaphore_signal(barrier, inc=1, device_id=(facing,), device_id_type=MESH)
+    pl.semaphore_wait(barrier, levels + 1 + relaying)
 
     def remote(source, target, send, recv, device):
         return pltpu.make_async_remote_copy(
@@ -112,9 +121,68 @@
     for b in range(4):
         own[1 - core, b] = joined(arrived[b])
 
-    def stage_copy(level, stride, block):
-        place = stage.at[level, (me // stride) % 2, block]
-        return remote(place, place, stage_send.at[level, block], stage_recv.at[level, block], partner(stride))
+    half = size // 2
+    side = (me // 2) % 2
+    neighbour = partner(2) if levels else me
+
+    def relayed(level):
+        return jnp.logical_and(level == levels - 1, relaying == 1)
+
+    def outer(level):
+        return jnp.logical_and(relayed(level), (me // (n // 2)) % 2 == (me // max(n // 4, 1)) % 2)
+
+    def place(level, slot, block, part):
+        return stage.at[level, slot, block, pl.ds(pl.multiple_of(part * half, half), half)]
+
+    def across(level, stride, block):
+        far = partner(stride)
+        if relaying:
+            far = jnp.where(relayed(level), facing, far)
+        part = jnp.where(level == 0, 1 - side, side)
+        where = place(level, (me // stride) % 2, block, part)
+        return remote(where, where, stage_send.at[level, block], stage_recv.at[level, block], far)
+
+    def across_rest(level, stride, block):
+        where = place(level, (me // stride) % 2, block, side)
+        return remote(where, where, pass_send.at[level, block], pass_recv.at[level, block], neighbour)
+
+    def passing(level, stride, block):
+        where = place(level, 1 - (me // stride) % 2, block, side)
+        return remote(where, where, pass_send.at[level, block], pass_recv.at[level, block], neighbour)
+
+    def relay(level, stride, block):
+        where = place(level, 1 - (me // stride) % 2, block, side)
+        return remote(where, where, relay_send.at[block], stage_recv.at[level, block], partner(n // 4))
+
+    def send(level, stride, block):
+        @pl.when(jnp.logical_not(outer(level)))
+        def _():
+            across(level, stride, block).start()
+
+        @pl.when(level == 0)
+        def _():
+            across_rest(level, stride, block).start()
+
+    def service(level, stride, block):
+        @pl.when(level < levels)
+        def _():
+            across(level, stride, block).wait_recv()
+
+            @pl.when(level > 0)
+            def _():
+                passing(level, stride, block).start()
+
+            if relaying:
+
+                @pl.when(jnp.logical_and(relayed(level), jnp.logical_not(outer(level))))
+                def _():
+                    relay(level, stride, block).start()
+
+    def finish(level, stride, block):
+        passing(level, stride, block).wait_recv()
+
+    def needed_first(stride):
+        return RIGHT * ((me // stride) % 2)
 
     def total_copy(k):
         return remote(
@@ -125,9 +193,15 @@
         def emit(block, value):
             stage[level, (me // stride) % 2, block] = value
 
-            @pl.when(level < levels)
-            def _():
-                stage_copy(level, stride, block).start()
+            if block != LEFT:
+
+                @pl.when(level < levels)
+                def _():
+                    if block == RIGHT:
+                        send(level, stride, RIGHT - needed_first(stride))
+                        send(level, stride, needed_first(stride))
+                    else:
+                        send(level, stride, block)
 
             if block in (LEFT, FORE):
 
@@ -152,19 +226,34 @@
     def climb(level, stride):
         lower, upper = stage.at[level, 0], stage.at[level, 1]
 
-        def wait_for(*blocks):
-            for block in blocks:
-                stage_copy(level, stride, block).wait_recv()
-
-        wait_for(LEFT, RIGHT)
-        star([(lower, upper, emit_stage(level + 1, 2 * stride))], work, lambda: wait_for(BACK, FORE))
+        following, doubled = level + 1, 2 * stride
+        finish(level, stride, needed_first(stride))
+
+        def late():
+            finish(level, stride, RIGHT - needed_first(stride))
+            finish(level, stride, BACK)
+            finish(level, stride, FORE)
+
+        star(
+            [(lower, upper, emit_stage(following, doubled))], work,
+            lambda: service(level, stride, BACK), lambda: service(level, stride, FORE), late,
+        )
+        first = lambda: service(following, doubled, needed_first(doubled))
 
         @pl.when((me // stride) % 2 == 1)
         def _():
-            star([(lower, before, emit_before)], work)
-
-        return 2 * stride
-
+            star([(lower, before, emit_before)], work, middle=first)
+
+        @pl.when((me // stride) % 2 == 0)
+        def _():
+            first()
+
+        service(following, doubled, RIGHT - needed_first(doubled))
+        return doubled
+
+    if levels:
+        service(0, 2, needed_first(2))
+        service(0, 2, RIGHT - needed_first(2))
     lax.fori_loop(0, levels, climb, jnp.int32(2))
 
     def probe(frequency, whole):
@@ -198,10 +287,21 @@
 
     def drain(level, stride):
         for block in range(4):
-            stage_copy(level, stride, block).wait_send()
+            @pl.when(jnp.logical_not(outer(level)))
+            def _():
+                across(level, stride, block).wait_send()
+
+            passing(level, stride, block).wait_send()
         return 2 * stride
 
     lax.fori_loop(0, levels, drain, jnp.int32(2))
+    if relaying:
+
+        @pl.when(jnp.logical_not(outer(levels - 1)))
+        def _():
+            for block in range(4):
+                relay(levels - 1, n // 2, block).wait_send()
+
     for block in range(4):
         out_copy(block).wait()
 
@@ -231,6 +331,9 @@
                 dma((2,)),
                 dma((max(levels, 1), 4)),
                 dma((max(levels, 1), 4)),
+                dma((max(levels, 1), 4)),
+                dma((max(levels, 1), 4)),
+                dma((4,)),
                 dma((2, 2)),
                 dma((4,)),
                 dma((4,)),

time: 88.8 us -> 81.4 us (0.917)
  Pallas kernels: 83.4 us -> 76.1 us
    pallas_call x1, Pallas kernels: 83.4 us -> 76.1 us  [local(): pl.pallas_call(functools.partial(kernel, n, levels), out_shape=tuple((jax...]
where the time goes in v1:
time: 81.4 us; the launch traced here: 81.2 us
  Pallas kernels  76.1 us (93%)
  local copies, waits for them, and re-layouts  4.54 us (6%)
    pallas_call x1, Pallas kernels, local(): pl.pallas_call(functools.partial(kernel, n, levels), out_shape=tuple((jax...  76.1 us
    unnamed x7, local copies, waits for them, and re-layouts  4.54 us

profile of v1, /device:TPU:25, one launch (start us, length us, event | category | flops | bytes accessed | tf_op | source)
XLA Modules:
  0.0 81.2 jit_solution(9871777153721952086)
XLA Ops:
  0.6 0.0 copy-start
  0.6 1.2 %copy-done = f32[1,2,4,2,128,128]{5,4,3,2,1,0:T(8,128)S(1)} copy-done((f32[1,2,4,2,128,128]{5,4,3,2,1,0:T(8,128)S(1)}, f32[1,2,4,2,128,128]{5,4,3,2,1,0:T(8,128)}, u32[]{:S(2)}) %copy-start) | copy-done | bytes 1048600
  1.9 0.0 copy-start.1
  1.9 0.9 %copy-done.1 = f32[2,2,128,128]{3,2,1,0:T(8,128)S(1)} copy-done((f32[2,2,128,128]{3,2,1,0:T(8,128)S(1)}, f32[2,2,128,128]{3,2,1,0:T(8,128)}, u32[]{:S(2)}) %copy-start.1) | copy-done | bytes 262168
  2.8 76.1 %shard_map.49 = (f32[1,2,4,2,128,128]{5,4,3,2,1,0:T(8,128)S(1)}, f32[2,2,128,128]{3,2,1,0:T(8,128)S(1)}, f32[2,2,128,128]{3,2,1,0:T(8,128)S(1)}) custom-call(f32[1,2,4,2,128,128]{5,4,3,2,1,0:T(8,128)S(1)} %copy-done, f32[2,2,128,128]{3,2,1,0:T(8,128)S(1)} %copy-done.1), custom_call_target="tpu_custom_call" | custom-call | tf_op jit(solution)/shard_map/pallas_call | solution.py:318
  78.9 1.0 %copy.8 = f32[1,2,4,2,128,128]{5,4,3,2,1,0:T(8,128)} copy(f32[1,2,4,2,128,128]{5,4,3,2,1,0:T(8,128)S(1)} %get-tuple-element.6) | data formatting | bytes 2097152
  79.8 0.7 copy.9
  80.5 0.7 copy.10
Async XLA Ops:
  0.6 1.2 %copy-start = (f32[1,2,4,2,128,128]{5,4,3,2,1,0:T(8,128)S(1)}, f32[1,2,4,2,128,128]{5,4,3,2,1,0:T(8,128)}, u32[]{:S(2)}) copy-start(f32[1,2,4,2,128,128]{5,4,3,2,1,0:T(8,128)} %sections.1) | copy-start | bytes 3145732
  1.9 0.9 %copy-start.1 = (f32[2,2,128,128]{3,2,1,0:T(8,128)S(1)}, f32[2,2,128,128]{3,2,1,0:T(8,128)}, u32[]{:S(2)}) copy-start(f32[2,2,128,128]{3,2,1,0:T(8,128)} %probes.1) | copy-start | bytes 786436
